TPU v7x, 32 devices: a whole 2x2x4 slice. The times are simulated.
32 devices in a mesh: dom: 32 (over z, y, x, core).
Axes of the slice: x: 2, y: 2, z: 4, core: 2. Of those that a mesh axis runs over, the one named last changes fastest.
Arguments:
- field: float32 [3, 180224], P(None, 'dom'), may hold values from -6 to 6
- blocks: bfloat16 [30, 30, 131072], P(None, None, 'dom'), may hold values from -1 to 1
- connectivity: int32 [10, 131072], P(None, 'dom'), may hold values from 0 to 8703, as said below
- send_nodes: int32 [8, 12288], P(None, 'dom'), may hold values from 0 to 5631
- live_blocks: int32 [32], replicated, may hold values from 1 to 8
Outputs:
- image: float32 [3, 180224], P(None, 'dom')
Inputs may be any that keep to these rules, and one draw needn't show every extreme that they name: `connectivity`: entries below 5632 name nodes of the element's own subdomain; entry 5632 + k * 384 + g names the node sent as entry g of row k by subdomain d - o_k, and only where that subdomain exists. `send_nodes`: columns d * 384 to (d + 1) * 384 - 1 of row k list local indices of nodes that subdomain d owns, in the order in which subdomain d + o_k numbers its ghost slots from d. Subdomain d's elements fill its first 512 * live_blocks[d] slots; the other slots are unused.
All inputs are finite; a program needn't handle non-finite values.
Results may differ from a plain program's by a relative error of at most 0.0003.
Values sent between devices are 32-bit elements; how exact they have to be, the bound alone decides.
A program may use at most 64 MiB of HBM per device.

v0:
```python
import jax
import jax.numpy as jnp
from jax import lax
from jax.sharding import PartitionSpec as P

BLK = 512


lanes = 128


def split_tables(indices, height):
    upper = indices // lanes
    lower = indices % lanes
    upper_hot = (
        lax.broadcasted_iota(jnp.int32, (height, indices.shape[0]), 0) == upper[None, :]
    ).astype(jnp.float32)
    lower_hot = (
        lax.broadcasted_iota(jnp.int32, (lanes, indices.shape[0]), 0) == lower[None, :]
    ).astype(jnp.float32)
    return (upper_hot, lower_hot)


def pick_columns(table, indices):
    height = table.shape[1] // lanes
    upper_hot, lower_hot = split_tables(indices, height)
    spread = jnp.dot(
        table.reshape(3 * height, lanes),
        lower_hot,
        precision=lax.Precision.HIGHEST,
        preferred_element_type=jnp.float32,
    )
    spread = spread.reshape(3, height, indices.shape[0])
    return jnp.sum(spread * upper_hot[None, :, :], axis=1)


def spread_columns(values, indices, width):
    height = width // lanes
    upper_hot, lower_hot = split_tables(indices, height)
    placed = (values[:, None, :] * upper_hot[None, :, :]).reshape(3 * height, indices.shape[0])
    summed = lax.dot_general(
        placed,
        lower_hot,
        (((1,), (1,)), ((), ())),
        precision=lax.Precision.HIGHEST,
        preferred_element_type=jnp.float32,
    )
    return summed.reshape(3, width)


def apply_blocks(stiffness, values):
    return jnp.sum(stiffness.astype(jnp.float32) * values[None, :, :], axis=1)


def body(field, blocks, connectivity, send_nodes, live_blocks):
    devices = lax.axis_size("dom")
    device = lax.axis_index("dom")
    owned_nodes = field.shape[1]
    bucket = send_nodes.shape[1]
    reach_count = send_nodes.shape[0] // 2
    block_len = BLK
    offsets = [k + 1 if k < reach_count else reach_count - 1 - k for k in range(2 * reach_count)]
    owned_width = -(-owned_nodes // lanes) * lanes
    send_flat = send_nodes.reshape(-1)
    outgoing = pick_columns(field, send_flat).reshape(3, 2 * reach_count, bucket)
    pieces = []
    buffer = jnp.zeros((devices, 3, bucket), jnp.float32)
    for k, o in enumerate(offsets):
        target = device + o
        inside = (target >= 0) & (target < devices)
        buffer = buffer.at[jnp.mod(target, devices)].add(jnp.where(inside, outgoing[:, k], 0.0))
    arrived = lax.all_to_all(buffer, "dom", split_axis=0, concat_axis=0, tiled=True)
    for k, o in enumerate(offsets):
        source = device - o
        inside = (source >= 0) & (source < devices)
        pieces.append(jnp.where(inside, arrived[jnp.mod(source, devices)], 0.0))
    nodal_table = jnp.concatenate([field] + pieces, axis=1)
    extended = nodal_table.shape[1]
    table_width = -(-extended // lanes) * lanes

    def block_step(b, running):
        element_nodes = lax.dynamic_slice_in_dim(connectivity, b * block_len, block_len, 1)
        stiffness = lax.dynamic_slice_in_dim(blocks, b * block_len, block_len, 2)
        flat_nodes = element_nodes.reshape(-1)
        values = pick_columns(nodal_table, flat_nodes).reshape(30, block_len)
        forces = apply_blocks(stiffness, values)
        return running + spread_columns(forces.reshape(3, 10 * block_len), flat_nodes, table_width)

    totals = jnp.zeros((3, table_width), jnp.float32)
    totals = lax.fori_loop(0, live_blocks[device], block_step, totals)
    partial_value = totals[:, owned_nodes:extended].reshape(3, 2 * reach_count, bucket)
    result = totals[:, :owned_nodes]
    returned = []
    buffer = jnp.zeros((devices, 3, bucket), jnp.float32)
    for k, o in enumerate(offsets):
        source = device - o
        inside = (source >= 0) & (source < devices)
        buffer = buffer.at[jnp.mod(source, devices)].add(
            jnp.where(inside, partial_value[:, k], 0.0)
        )
    returned_sums = lax.all_to_all(buffer, "dom", split_axis=0, concat_axis=0, tiled=True)
    for k, o in enumerate(offsets):
        target = device + o
        inside = (target >= 0) & (target < devices)
        returned.append(jnp.where(inside, returned_sums[jnp.mod(target, devices)], 0.0))
    incoming = jnp.concatenate(returned, axis=1)
    added = spread_columns(incoming, send_flat, owned_width)
    return result + added


def solution(mesh):
    return jax.shard_map(
        body,
        mesh=mesh,
        in_specs=(P(None, "dom"), P(None, None, "dom"), P(None, "dom"), P(None, "dom"), P()),
        out_specs=P(None, "dom"),
        check_vma=False,
    )
```

profile of v0, /device:TPU:1, one launch (start us, length us, event | category | flops | bytes accessed | tf_op | source)
XLA Modules:
  0.0 260.7 jit_solution(6986581789767644575)
XLA Ops:
  20.1 7.1 %all-to-all-start = ((f32[32,3,384]{2,1,0:T(4,128)}), f32[32,3,384]{2,1,0:T(4,128)S(1)}, u32[]{:S(2)}, u32[]{:S(2)}) async-start(f32[32,3,384]{2,1,0:T(4,128)} %constant_dynamic-update-slice_fusion.25), calls=%async_computation | async-start | bytes 393216 | tf_op jit(solution)/shard_map/all_to_all | solution.py:72
  27.8 8.6 %all-to-all-done = f32[32,3,384]{2,1,0:T(4,128)S(1)} async-done(((f32[32,3,384]{2,1,0:T(4,128)}), f32[32,3,384]{2,1,0:T(4,128)S(1)}, u32[]{:S(2)}, u32[]{:S(2)}) %all-to-all-start) | async-done | bytes 147488 | tf_op jit(solution)/shard_map/all_to_all | solution.py:72
  37.2 152.2 %while.29 = (s32[]{:T(128)}, f32[3,8704]{1,0:T(4,128)S(1)}, s32[]{:T(128)}, bf16[30,30,4096]{2,1,0:T(8,128)(2,1)}, s32[10,4096]{1,0:T(8,128)}, /*index=5*/f32[3,...) while((s32[]{:T(128)}, f32[3,8704]{1,0:T(4,128)S(1)}, ...), condition=%wide.wide.region_12.13_spmd, body=%wide.wide.region_9.12_spmd.sunk | while | flops 3215258112 | bytes 39950496 | solution.py:90
  38.6 3.8 %convolution_bitcast_fusion.4 = f32[204,5120]{1,0:T(8,128)} fusion(f32[204,128]{1,0:T(8,128)S(1)} %get-tuple-element.412, s32[5120]{0:T(1024)S(1)} %get-tuple-element.382), kind=kOutput, calls=%fused_computation.clone.clone.1 | convolution fusion | flops 1604976640 | bytes 4302848 | tf_op jit(solution)/shard_map/while/body/dot_general | solution.py:27
  42.4 4.1 %reshape.904 = f32[3,68,5120]{2,1,0:T(8,128)} reshape(f32[204,5120]{1,0:T(8,128)} %convolution_bitcast_fusion.4) | data formatting | bytes 8355840 | tf_op jit(solution)/shard_map/while/body/reshape | solution.py:33
  46.6 2.9 %multiply_reduce_fusion.7 = f32[3,5120]{1,0:T(4,128)S(1)} fusion(f32[3,68,5120]{2,1,0:T(8,128)} %reshape.904, f32[68,5120]{1,0:T(8,128)S(1)} %fusion.76), kind=kLoop, calls=%fused_computation.1.clone.clone.1 | loop fusion | flops 2073600 | bytes 5632000 | tf_op jit(solution)/shard_map/while/body/reduce_sum | solution.py:34
  53.6 4.1 %mul.136 = f32[204,5120]{1,0:T(8,128)} reshape(f32[3,68,5120]{2,1,0:T(8,128)} %broadcast_multiply_fusion.4) | data formatting | bytes 8355840 | tf_op jit(solution)/shard_map/while/body/mul | solution.py:40
  57.8 4.6 %fusion.77 = f32[204,128]{1,0:T(8,128)S(1)} fusion(f32[204,5120]{1,0:T(8,128)} %mul.136, s32[5120]{0:T(1024)S(1)} %get-tuple-element.382), kind=kOutput, calls=%fused_computation.3.clone.clone.1 | convolution fusion | flops 1604976640 | bytes 4302848 | tf_op jit(solution)/shard_map/while/body/dot_general | solution.py:41
  63.8 3.8 %convolution_bitcast_fusion.4 = f32[204,5120]{1,0:T(8,128)} fusion(f32[204,128]{1,0:T(8,128)S(1)} %get-tuple-element.412, s32[5120]{0:T(1024)S(1)} %get-tuple-element.382), kind=kOutput, calls=%fused_computation.clone.clone.1 | convolution fusion | flops 1604976640 | bytes 4302848 | tf_op jit(solution)/shard_map/while/body/dot_general | solution.py:27
  67.7 4.1 %reshape.904 = f32[3,68,5120]{2,1,0:T(8,128)} reshape(f32[204,5120]{1,0:T(8,128)} %convolution_bitcast_fusion.4) | data formatting | bytes 8355840 | tf_op jit(solution)/shard_map/while/body/reshape | solution.py:33
  71.9 2.9 %multiply_reduce_fusion.7 = f32[3,5120]{1,0:T(4,128)S(1)} fusion(f32[3,68,5120]{2,1,0:T(8,128)} %reshape.904, f32[68,5120]{1,0:T(8,128)S(1)} %fusion.76), kind=kLoop, calls=%fused_computation.1.clone.clone.1 | loop fusion | flops 2073600 | bytes 5632000 | tf_op jit(solution)/shard_map/while/body/reduce_sum | solution.py:34
  78.9 4.1 %mul.136 = f32[204,5120]{1,0:T(8,128)} reshape(f32[3,68,5120]{2,1,0:T(8,128)} %broadcast_multiply_fusion.4) | data formatting | bytes 8355840 | tf_op jit(solution)/shard_map/while/body/mul | solution.py:40
  83.0 4.6 %fusion.77 = f32[204,128]{1,0:T(8,128)S(1)} fusion(f32[204,5120]{1,0:T(8,128)} %mul.136, s32[5120]{0:T(1024)S(1)} %get-tuple-element.382), kind=kOutput, calls=%fused_computation.3.clone.clone.1 | convolution fusion | flops 1604976640 | bytes 4302848 | tf_op jit(solution)/shard_map/while/body/dot_general | solution.py:41
  89.1 3.8 %convolution_bitcast_fusion.4 = f32[204,5120]{1,0:T(8,128)} fusion(f32[204,128]{1,0:T(8,128)S(1)} %get-tuple-element.412, s32[5120]{0:T(1024)S(1)} %get-tuple-element.382), kind=kOutput, calls=%fused_computation.clone.clone.1 | convolution fusion | flops 1604976640 | bytes 4302848 | tf_op jit(solution)/shard_map/while/body/dot_general | solution.py:27
  93.0 4.1 %reshape.904 = f32[3,68,5120]{2,1,0:T(8,128)} reshape(f32[204,5120]{1,0:T(8,128)} %convolution_bitcast_fusion.4) | data formatting | bytes 8355840 | tf_op jit(solution)/shard_map/while/body/reshape | solution.py:33
  97.2 2.9 %multiply_reduce_fusion.7 = f32[3,5120]{1,0:T(4,128)S(1)} fusion(f32[3,68,5120]{2,1,0:T(8,128)} %reshape.904, f32[68,5120]{1,0:T(8,128)S(1)} %fusion.76), kind=kLoop, calls=%fused_computation.1.clone.clone.1 | loop fusion | flops 2073600 | bytes 5632000 | tf_op jit(solution)/shard_map/while/body/reduce_sum | solution.py:34
  104.2 4.1 %mul.136 = f32[204,5120]{1,0:T(8,128)} reshape(f32[3,68,5120]{2,1,0:T(8,128)} %broadcast_multiply_fusion.4) | data formatting | bytes 8355840 | tf_op jit(solution)/shard_map/while/body/mul | solution.py:40
  108.3 4.6 %fusion.77 = f32[204,128]{1,0:T(8,128)S(1)} fusion(f32[204,5120]{1,0:T(8,128)} %mul.136, s32[5120]{0:T(1024)S(1)} %get-tuple-element.382), kind=kOutput, calls=%fused_computation.3.clone.clone.1 | convolution fusion | flops 1604976640 | bytes 4302848 | tf_op jit(solution)/shard_map/while/body/dot_general | solution.py:41
  114.4 3.8 %convolution_bitcast_fusion.4 = f32[204,5120]{1,0:T(8,128)} fusion(f32[204,128]{1,0:T(8,128)S(1)} %get-tuple-element.412, s32[5120]{0:T(1024)S(1)} %get-tuple-element.382), kind=kOutput, calls=%fused_computation.clone.clone.1 | convolution fusion | flops 1604976640 | bytes 4302848 | tf_op jit(solution)/shard_map/while/body/dot_general | solution.py:27
  118.2 4.1 %reshape.904 = f32[3,68,5120]{2,1,0:T(8,128)} reshape(f32[204,5120]{1,0:T(8,128)} %convolution_bitcast_fusion.4) | data formatting | bytes 8355840 | tf_op jit(solution)/shard_map/while/body/reshape | solution.py:33
  129.4 4.1 %mul.136 = f32[204,5120]{1,0:T(8,128)} reshape(f32[3,68,5120]{2,1,0:T(8,128)} %broadcast_multiply_fusion.4) | data formatting | bytes 8355840 | tf_op jit(solution)/shard_map/while/body/mul | solution.py:40
  133.6 4.6 %fusion.77 = f32[204,128]{1,0:T(8,128)S(1)} fusion(f32[204,5120]{1,0:T(8,128)} %mul.136, s32[5120]{0:T(1024)S(1)} %get-tuple-element.382), kind=kOutput, calls=%fused_computation.3.clone.clone.1 | convolution fusion | flops 1604976640 | bytes 4302848 | tf_op jit(solution)/shard_map/while/body/dot_general | solution.py:41
  139.6 3.8 %convolution_bitcast_fusion.4 = f32[204,5120]{1,0:T(8,128)} fusion(f32[204,128]{1,0:T(8,128)S(1)} %get-tuple-element.412, s32[5120]{0:T(1024)S(1)} %get-tuple-element.382), kind=kOutput, calls=%fused_computation.clone.clone.1 | convolution fusion | flops 1604976640 | bytes 4302848 | tf_op jit(solution)/shard_map/while/body/dot_general | solution.py:27
  143.5 4.1 %reshape.904 = f32[3,68,5120]{2,1,0:T(8,128)} reshape(f32[204,5120]{1,0:T(8,128)} %convolution_bitcast_fusion.4) | data formatting | bytes 8355840 | tf_op jit(solution)/shard_map/while/body/reshape | solution.py:33
  147.7 2.9 %multiply_reduce_fusion.7 = f32[3,5120]{1,0:T(4,128)S(1)} fusion(f32[3,68,5120]{2,1,0:T(8,128)} %reshape.904, f32[68,5120]{1,0:T(8,128)S(1)} %fusion.76), kind=kLoop, calls=%fused_computation.1.clone.clone.1 | loop fusion | flops 2073600 | bytes 5632000 | tf_op jit(solution)/shard_map/while/body/reduce_sum | solution.py:34
  154.7 4.1 %mul.136 = f32[204,5120]{1,0:T(8,128)} reshape(f32[3,68,5120]{2,1,0:T(8,128)} %broadcast_multiply_fusion.4) | data formatting | bytes 8355840 | tf_op jit(solution)/shard_map/while/body/mul | solution.py:40
  158.8 4.6 %fusion.77 = f32[204,128]{1,0:T(8,128)S(1)} fusion(f32[204,5120]{1,0:T(8,128)} %mul.136, s32[5120]{0:T(1024)S(1)} %get-tuple-element.382), kind=kOutput, calls=%fused_computation.3.clone.clone.1 | convolution fusion | flops 1604976640 | bytes 4302848 | tf_op jit(solution)/shard_map/while/body/dot_general | solution.py:41
  164.9 3.8 %convolution_bitcast_fusion.4 = f32[204,5120]{1,0:T(8,128)} fusion(f32[204,128]{1,0:T(8,128)S(1)} %get-tuple-element.412, s32[5120]{0:T(1024)S(1)} %get-tuple-element.382), kind=kOutput, calls=%fused_computation.clone.clone.1 | convolution fusion | flops 1604976640 | bytes 4302848 | tf_op jit(solution)/shard_map/while/body/dot_general | solution.py:27
  168.8 4.1 %reshape.904 = f32[3,68,5120]{2,1,0:T(8,128)} reshape(f32[204,5120]{1,0:T(8,128)} %convolution_bitcast_fusion.4) | data formatting | bytes 8355840 | tf_op jit(solution)/shard_map/while/body/reshape | solution.py:33
  180.0 4.1 %mul.136 = f32[204,5120]{1,0:T(8,128)} reshape(f32[3,68,5120]{2,1,0:T(8,128)} %broadcast_multiply_fusion.4) | data formatting | bytes 8355840 | tf_op jit(solution)/shard_map/while/body/mul | solution.py:40
  184.1 4.6 %fusion.77 = f32[204,128]{1,0:T(8,128)S(1)} fusion(f32[204,5120]{1,0:T(8,128)} %mul.136, s32[5120]{0:T(1024)S(1)} %get-tuple-element.382), kind=kOutput, calls=%fused_computation.3.clone.clone.1 | convolution fusion | flops 1604976640 | bytes 4302848 | tf_op jit(solution)/shard_map/while/body/dot_general | solution.py:41
  194.4 61.4 %all_to_all.10 = f32[32,3,384]{2,1,0:T(4,128)S(1)} all-to-all(f32[32,3,384]{2,1,0:T(4,128)S(1)} %constant_dynamic-update-slice_fusion.17), channel_id=1, replica_groups=mesh['dom'=32] {'dom'}, dimensions={0} | all-to-all | bytes 294912 | tf_op jit(solution)/shard_map/all_to_all | solution.py:101
  (123 shorter events, 67.6 us)
Async XLA Ops:
  2.8 0.7 copy-start.2
  2.8 24.4 %copy-start.1 = (f32[3,5632]{1,0:T(4,128)S(1)}, f32[3,5632]{1,0:T(4,128)}, u32[]{:S(2)}) copy-start(f32[3,5632]{1,0:T(4,128)} %param.39) | copy-start | bytes 202756
  2.8 24.4 %copy-start.3 = (s32[32]{0:T(128)S(1)}, s32[32]{0:T(128)}, u32[]{:S(2)}) copy-start(s32[32]{0:T(128)} %param.43) | copy-start | bytes 388
  20.1 16.3 %all-to-all-start = ((f32[32,3,384]{2,1,0:T(4,128)}), f32[32,3,384]{2,1,0:T(4,128)S(1)}, u32[]{:S(2)}, u32[]{:S(2)}) async-start(f32[32,3,384]{2,1,0:T(4,128)} %constant_dynamic-update-slice_fusion.25), calls=%async_computation | async-start | bytes 393216 | tf_op jit(solution)/shard_map/all_to_all | solution.py:72
  36.5 0.7 copy-start
where the time goes:
time: 263 us; the launch traced here: 261 us
  other arithmetic  64.9 us (25%)
  blocking collectives  61.4 us (23%)
  local copies, waits for them, and re-layouts  60 us (23%)
  matrix products  54.1 us (21%)
  waiting for transfers between devices  8.6 us (3%)
  starting transfers between devices  7.08 us (3%)
  loops' own time  4.27 us (2%)
    all_to_all x1, blocking collectives, body(): lax.all_to_all(buffer, 'dom', split_axis=0, concat_axis=0, tiled=True)  61.4 us
    dot_general x7, matrix products, spread_columns(): lax.dot_general(placed, lower_hot, (((1,), (1,)), ((), ())), precision=la...  30.2 us
    mul x13, local copies, waits for them, and re-layouts, spread_columns(): values[:, None, :] * upper_hot[None, :, :]  26.3 us
    reshape x7, local copies, waits for them, and re-layouts, pick_columns(): spread = spread.reshape(3, height, indices.shape[0])  24.7 us
    dot_general x7, matrix products, pick_columns(): jnp.dot(table.reshape(3 * height, lanes), lower_hot, precision=lax.Precis...  23.9 us
    reduce_sum x7, other arithmetic, pick_columns(): return jnp.sum(spread * upper_hot[None, :, :], axis=1)  17.5 us
    mul x7, other arithmetic, spread_columns(): values[:, None, :] * upper_hot[None, :, :]  15.3 us
    scatter-add x8, other arithmetic, body(): buffer.at[jnp.mod(target, devices)]  14.4 us
  transfers between devices with their start and end apart: 1, of which 1 were waited for; matrix products, arithmetic and copies ran while one was open for 0% of the time, Pallas kernels for 0%

commit v1 on v0

v1 whole, which is shorter than its diff:
```python
import functools

import jax
import jax.numpy as jnp
from jax import lax
from jax.experimental import pallas as pl
from jax.experimental.pallas import tpu as pltpu
from jax.sharding import PartitionSpec as P

BLK = 512
LOW = 256
LANES = 128
MESH = pl.DeviceIdType.MESH
VM = pl.BlockSpec(memory_space=pltpu.VMEM)


def round_up(n, m):
    return -(-n // m) * m


def split_parts(x):
    high = x.astype(jnp.bfloat16)
    low = (x - high.astype(jnp.float32)).astype(jnp.bfloat16)
    return high, low


def lower_hot(indices):
    lower = jnp.bitwise_and(indices, LOW - 1)
    rows = lax.broadcasted_iota(jnp.int32, (LOW, indices.shape[1]), 0)
    return jnp.where(rows == lower, 1.0, 0.0).astype(jnp.bfloat16)


def upper_mask(indices, height):
    upper = jnp.right_shift(indices, LOW.bit_length() - 1)
    return lax.broadcasted_iota(jnp.int32, (height, indices.shape[1]), 0) == upper


def pick(parts, hot, mask, height):
    spread = jnp.dot(parts, hot, preferred_element_type=jnp.float32)
    rows = []
    for c in range(3):
        whole = spread[c * height:(c + 1) * height] + spread[(3 + c) * height:(4 + c) * height]
        rows.append(jnp.sum(jnp.where(mask, whole, 0.0), axis=0, keepdims=True))
    return rows


def spread_back(rows, hot, mask):
    pairs = [split_parts(row) for row in rows]
    stacked = [jnp.where(mask, pair[p].astype(jnp.float32), 0.0) for p in range(2) for pair in pairs]
    placed = jnp.concatenate(stacked, axis=0).astype(jnp.bfloat16)
    return lax.dot_general(
        placed, hot, (((1,), (1,)), ((), ())), preferred_element_type=jnp.float32
    )


def put_segments(table, height, first, source, c, width):
    for t in range(width // LANES):
        s = first + t
        row, col = c * height + s * LANES // LOW, s * LANES % LOW
        table[row:row + 1, col:col + LANES] = source(t)


def make_parts(table):
    high, low = split_parts(table[...])
    return jnp.concatenate([high, low], axis=0)


def pick_kernel(height, field_ref, send_ref, out_ref, table):
    nodes = field_ref.shape[1]
    table[...] = jnp.zeros_like(table)
    for c in range(3):
        put_segments(
            table, height, 0, lambda t: field_ref[c:c + 1, t * LANES:(t + 1) * LANES], c, nodes
        )
    parts = make_parts(table)
    for k in range(send_ref.shape[0]):
        indices = send_ref[k:k + 1, :]
        rows = pick(parts, lower_hot(indices), upper_mask(indices, height), height)
        for c in range(3):
            out_ref[k, c:c + 1, :] = rows[c]


def exchange_kernel(sign, devices, offsets, in_ref, out_ref, send_sem, recv_sem):
    me = lax.axis_index("dom")
    barrier = pltpu.get_barrier_semaphore()
    count = 0
    for o in offsets:
        other = me + o
        inside = (other >= 0) & (other < devices)
        count = count + inside.astype(jnp.int32)

        @pl.when(inside)
        def _():
            pl.semaphore_signal(barrier, inc=1, device_id=(other,), device_id_type=MESH)

    pl.semaphore_wait(barrier, count)

    def copy_of(k):
        return pltpu.make_async_remote_copy(
            src_ref=in_ref.at[k],
            dst_ref=out_ref.at[k],
            send_sem=send_sem.at[k],
            recv_sem=recv_sem.at[k],
            device_id=(me + sign * offsets[k],),
            device_id_type=MESH,
        )

    def inside_of(k, way):
        other = me + way * sign * offsets[k]
        return (other >= 0) & (other < devices)

    order = sorted(range(len(offsets)), key=lambda k: -abs(offsets[k]))
    for k in order:

        @pl.when(inside_of(k, 1))
        def _():
            copy_of(k).start()

    for k in order:

        @pl.when(jnp.logical_not(inside_of(k, -1)))
        def _():
            out_ref[k] = jnp.zeros(out_ref.shape[1:], jnp.float32)

    for k in order:

        @pl.when(inside_of(k, 1))
        def _():
            copy_of(k).wait_send()

        @pl.when(inside_of(k, -1))
        def _():
            copy_of(k).wait_recv()


def exchange(values, sign, devices, offsets):
    return pl.pallas_call(
        functools.partial(exchange_kernel, sign, devices, offsets),
        out_shape=jax.ShapeDtypeStruct(values.shape, jnp.float32),
        in_specs=[VM],
        out_specs=VM,
        scratch_shapes=[
            pltpu.SemaphoreType.DMA((len(offsets),)),
            pltpu.SemaphoreType.DMA((len(offsets),)),
        ],
        compiler_params=pltpu.CompilerParams(
            collective_id=0 if sign > 0 else 1, has_side_effects=True
        ),
        name="exchange_out" if sign > 0 else "exchange_back",
    )(values)


def element_kernel(
    height, live_ref, field_ref, ghost_ref, conn_ref, block_ref, owned_ref, back_ref,
    table, parts, total, values,
):
    step = pl.program_id(0)
    nodes = field_ref.shape[1]
    reach, _, bucket = ghost_ref.shape

    @pl.when(step == 0)
    def _():
        table[...] = jnp.zeros_like(table)
        total[...] = jnp.zeros_like(total)
        for c in range(3):
            put_segments(
                table, height, 0, lambda t: field_ref[c:c + 1, t * LANES:(t + 1) * LANES], c, nodes
            )
            for k in range(reach):
                put_segments(
                    table, height, (nodes + k * bucket) // LANES,
                    lambda t: ghost_ref[k, c:c + 1, t * LANES:(t + 1) * LANES], c, bucket,
                )
        parts[...] = make_parts(table)

    @pl.when(step < live_ref[lax.axis_index("dom")])
    def _():
        corners = conn_ref.shape[0]
        for a in range(corners):
            indices = conn_ref[a:a + 1, :]
            rows = pick(parts[...], lower_hot(indices), upper_mask(indices, height), height)
            for c in range(3):
                values[c * corners + a:c * corners + a + 1, :] = rows[c]
        v = values[...]
        forces = [
            jnp.sum(block_ref[i].astype(jnp.float32) * v, axis=0, keepdims=True)
            for i in range(3 * corners)
        ]
        for a in range(corners):
            indices = conn_ref[a:a + 1, :]
            total[...] += spread_back(
                [forces[c * corners + a] for c in range(3)],
                lower_hot(indices),
                upper_mask(indices, height),
            )

    @pl.when(step == pl.num_programs(0) - 1)
    def _():
        table[...] = total[:3 * height, :] + total[3 * height:, :]

        def segment(c, s):
            row, col = c * height + s * LANES // LOW, s * LANES % LOW
            return table[row:row + 1, col:col + LANES]

        for c in range(3):
            for t in range(nodes // LANES):
                owned_ref[c:c + 1, t * LANES:(t + 1) * LANES] = segment(c, t)
            for k in range(reach):
                for t in range(bucket // LANES):
                    back_ref[k, c:c + 1, t * LANES:(t + 1) * LANES] = segment(
                        c, (nodes + k * bucket) // LANES + t
                    )


def add_kernel(height, owned_ref, in_ref, send_ref, out_ref, total):
    nodes = owned_ref.shape[1]
    acc = jnp.zeros((6 * height, LOW), jnp.float32)
    for k in range(send_ref.shape[0]):
        indices = send_ref[k:k + 1, :]
        acc = acc + spread_back(
            [in_ref[k, c:c + 1, :] for c in range(3)],
            lower_hot(indices),
            upper_mask(indices, height),
        )
    total[...] = acc[:3 * height] + acc[3 * height:]
    for c in range(3):
        for t in range(nodes // LANES):
            row, col = c * height + t * LANES // LOW, t * LANES % LOW
            span = slice(t * LANES, (t + 1) * LANES)
            out_ref[c:c + 1, span] = owned_ref[c:c + 1, span] + total[row:row + 1, col:col + LANES]


def body(field, blocks, connectivity, send_nodes, live_blocks):
    devices = lax.axis_size("dom")
    nodes = field.shape[1]
    reach2, bucket = send_nodes.shape
    reach = reach2 // 2
    offsets = [k + 1 if k < reach else reach - 1 - k for k in range(reach2)]
    corners, elements = connectivity.shape
    dofs = 3 * corners
    own_height = round_up(-(-nodes // LOW), 8)
    full_height = round_up(-(-(nodes + reach2 * bucket) // LOW), 8)
    ghost_shape = jax.ShapeDtypeStruct((reach2, 3, bucket), jnp.float32)
    field_shape = jax.ShapeDtypeStruct((3, nodes), jnp.float32)

    outgoing = pl.pallas_call(
        functools.partial(pick_kernel, own_height),
        out_shape=ghost_shape,
        in_specs=[VM, VM],
        out_specs=VM,
        scratch_shapes=[pltpu.VMEM((3 * own_height, LOW), jnp.float32)],
        name="pick_sent",
    )(field, send_nodes)
    ghosts = exchange(outgoing, 1, devices, offsets)

    whole = lambda *shape: pl.BlockSpec(shape, lambda b, live: (0,) * len(shape))
    owned, back = pl.pallas_call(
        functools.partial(element_kernel, full_height),
        out_shape=(field_shape, ghost_shape),
        grid_spec=pltpu.PrefetchScalarGridSpec(
            num_scalar_prefetch=1,
            grid=(elements // BLK,),
            in_specs=[
                whole(3, nodes),
                whole(reach2, 3, bucket),
                pl.BlockSpec((corners, BLK), lambda b, live: (0, b)),
                pl.BlockSpec((dofs, dofs, BLK), lambda b, live: (0, 0, b)),
            ],
            out_specs=[whole(3, nodes), whole(reach2, 3, bucket)],
            scratch_shapes=[
                pltpu.VMEM((3 * full_height, LOW), jnp.float32),
                pltpu.VMEM((6 * full_height, LOW), jnp.bfloat16),
                pltpu.VMEM((6 * full_height, LOW), jnp.float32),
                pltpu.VMEM((dofs, BLK), jnp.float32),
            ],
        ),
        compiler_params=pltpu.CompilerParams(dimension_semantics=("arbitrary",)),
        name="elements",
    )(live_blocks, field, ghosts, connectivity, blocks)

    returned = exchange(back, -1, devices, offsets)
    return pl.pallas_call(
        functools.partial(add_kernel, own_height),
        out_shape=field_shape,
        in_specs=[VM, VM, VM],
        out_specs=VM,
        scratch_shapes=[pltpu.VMEM((3 * own_height, LOW), jnp.float32)],
        name="add_returned",
    )(owned, returned, send_nodes)


def solution(mesh):
    return jax.shard_map(
        body,
        mesh=mesh,
        in_specs=(P(None, "dom"), P(None, None, "dom"), P(None, "dom"), P(None, "dom"), P()),
        out_specs=P(None, "dom"),
        check_vma=False,
    )
```

time: 263 us -> 42.1 us (0.16)
  other arithmetic: 64.9 us -> 0 us
  blocking collectives: 61.4 us -> 0 us
  local copies, waits for them, and re-layouts: 60 us -> 0 us
  matrix products: 54.1 us -> 0 us
  Pallas kernels: 0 us -> 41.3 us
  waiting for transfers between devices: 8.6 us -> 0 us
  starting transfers between devices: 7.08 us -> 0 us
  loops' own time: 4.27 us -> 0 us
    all_to_all x1 -> x0, blocking collectives: 61.4 us -> none  [body(): lax.all_to_all(buffer, 'dom', split_axis=0, concat_axis=0, tiled=True)]
    dot_general x14 -> x0, matrix products: 54.1 us -> none  [the longest x7 30.2 us: spread_columns(): lax.dot_general(placed, lower_hot, (((1,), (1,)), ((), ())), precision=la...]
    pallas_call x0 -> x5, Pallas kernels: none -> 41.3 us  [the longest x1 18.7 us: body(): pl.pallas_call(functools.partial(element_kernel, full_height), out_shape=...]
    reshape x23 -> x0, local copies, waits for them, and re-layouts: 26.7 us -> none  [the longest x7 24.7 us: pick_columns(): spread = spread.reshape(3, height, indices.shape[0])]
    reduce_sum x13 -> x0, other arithmetic: 26.6 us -> none  [the longest x7 17.5 us: pick_columns(): return jnp.sum(spread * upper_hot[None, :, :], axis=1)]
    mul x19 -> x0, local copies, waits for them, and re-layouts: 26.5 us -> none  [the longest x13 26.3 us: spread_columns(): values[:, None, :] * upper_hot[None, :, :]]
    scatter-add x16 -> x0, other arithmetic: 19.4 us -> none  [the longest x8 14.4 us: body(): buffer.at[jnp.mod(target, devices)]]
    mul x7 -> x0, other arithmetic: 15.3 us -> none  [spread_columns(): values[:, None, :] * upper_hot[None, :, :]]
  transfers between devices with their start and end apart: 1 -> 0, of which waited for: 1 -> 0; matrix products, arithmetic and copies ran while one was open for 0% -> 0% of each run, Pallas kernels for 0% -> 0%
where the time goes in v1:
time: 42.1 us; the launch traced here: 41.3 us
  Pallas kernels  41.3 us (98%)
    pallas_call x1, Pallas kernels, body(): pl.pallas_call(functools.partial(element_kernel, full_height), out_shape=...  18.7 us
    pallas_call x2, Pallas kernels, exchange(): pl.pallas_call(functools.partial(exchange_kernel, sign, devices, offsets)...  18.1 us
    pallas_call x1, Pallas kernels, body(): pl.pallas_call(functools.partial(add_kernel, own_height), out_shape=field...  2.25 us
    pallas_call x1, Pallas kernels, body(): pl.pallas_call(functools.partial(pick_kernel, own_height), out_shape=ghos...  2.16 us

profile of v1, /device:TPU:1, one launch (start us, length us, event | category | flops | bytes accessed | tf_op | source)
XLA Modules:
  0.0 41.3 jit_solution(5829689169485508101)
XLA Ops:
  0.0 2.2 %pick_sent.1.in_ref = f32[8,3,384]{2,1,0:T(4,128)} custom-call(f32[3,5632]{1,0:T(4,128)} %field_ref.3, s32[8,384]{1,0:T(8,128)} %send_ref.3), custom_call_target="tpu_custom_call" | custom-call | tf_op jit(solution)/shard_map/pick_sent/pallas_call | solution.py:246
  2.2 7.4 %exchange_out.1.ghost_ref = f32[8,3,384]{2,1,0:T(4,128)} custom-call(f32[8,3,384]{2,1,0:T(4,128)} %pick_sent.1.in_ref), custom_call_target="tpu_custom_call" | custom-call | tf_op jit(solution)/shard_map/exchange_out/pallas_call | solution.py:137
  9.6 18.7 %elements.1 = (f32[3,5632]{1,0:T(4,128)}, f32[8,3,384]{2,1,0:T(4,128)}) custom-call(s32[32]{0:T(128)} %live_ref.1, f32[3,5632]{1,0:T(4,128)} %field_ref.3, f32[8,3,384]{2,1,0:T(4,128)} %exchange_out.1.ghost_ref, s32[10,4096]{1,0:T(8,128)} %conn_ref.1, bf16[30,30,4096]{2,1,0:T(8,128)(2,1)} %block_ref.1), custom_call_target="tpu_custom_call" | custom-call | tf_op jit(solution)/shard_map/elements/pallas_call | solution.py:257
  28.3 10.7 %exchange_back.1.in_ref = f32[8,3,384]{2,1,0:T(4,128)} custom-call(f32[8,3,384]{2,1,0:T(4,128)} %get-tuple-element.8.in_ref), custom_call_target="tpu_custom_call" | custom-call | tf_op jit(solution)/shard_map/exchange_back/pallas_call | solution.py:137
  39.0 2.2 %add_returned.1 = f32[3,5632]{1,0:T(4,128)} custom-call(f32[3,5632]{1,0:T(4,128)} %get-tuple-element.7.owned_ref, f32[8,3,384]{2,1,0:T(4,128)} %exchange_back.1.in_ref, s32[8,384]{1,0:T(8,128)} %send_ref.3), custom_call_target="tpu_custom_call" | custom-call | tf_op jit(solution)/shard_map/add_returned/pallas_call | solution.py:282
